TPU v7x, 32 devices: a whole 2x2x4 slice. The times are simulated.
32 devices in a mesh: inner: 2 (over y), outer: 4 (over z), head: 4 (over x, core).
Axes of the slice: x: 2, y: 2, z: 4, core: 2. Of those that a mesh axis runs over, the one named last changes fastest.
Arguments:
- queries: bfloat16 [2048, 64, 128], P(('inner', 'outer', 'head')), may hold values from -6 to 6
- key_vector_rows: bfloat16 [2048, 8, 128], P(('inner', 'outer'), 'head'), may hold values from -6 to 6
- value_vector_rows: bfloat16 [2048, 8, 128], P(('inner', 'outer'), 'head'), may hold values from -6 to 6
- grad_out: bfloat16 [2048, 64, 128], P(('inner', 'outer', 'head')), may hold values from -24 to 24
Outputs:
- query_grads: bfloat16 [2048, 64, 128], P(('inner', 'outer', 'head'))
- key_gradient_rows: bfloat16 [2048, 8, 128], P(('inner', 'outer'), 'head')
- value_gradient_rows: bfloat16 [2048, 8, 128], P(('inner', 'outer'), 'head')
All inputs are finite; a program needn't handle non-finite values.
Results may differ from a plain program's by a relative error of at most 0.012.
Values may be sent and summed in bfloat16 or wider, within the bound.
No kernel may reach another device: no remote copies, remote signals or barrier semaphores. Data moves between devices by JAX's collectives and lax.ppermute only.
A program may use at most 64 MiB of HBM per device.

v0:
```python
import jax
import jax.numpy as jnp
from jax import lax
from jax.sharding import PartitionSpec as P


def from_behind(value, axis, by):
    peers = lax.axis_size(axis)
    pairs = [(i, i + by) for i in range(peers) if 0 <= i + by < peers]
    return lax.ppermute(value, axis, pairs)


def head_grads(query_part, grad_part, key_part, value_part, allowed):
    softmax_scale = query_part.shape[-1] ** (-0.5)
    scores = (
        jnp.einsum("rgd,kd->grk", query_part, key_part, preferred_element_type=jnp.float32)
        * softmax_scale
    )
    scores = jnp.where(allowed[None], scores, -jnp.inf)
    highest = jnp.max(scores, axis=-1, keepdims=True)
    probs = jnp.exp(scores - highest)
    probs = probs / jnp.sum(probs, axis=-1, keepdims=True)
    probs_low = probs.astype(jnp.bfloat16)
    value_gradient_rows = jnp.einsum(
        "grk,rgd->kd", probs_low, grad_part, preferred_element_type=jnp.float32
    )
    dprobs = jnp.einsum("rgd,kd->grk", grad_part, value_part, preferred_element_type=jnp.float32)
    delta = jnp.sum(probs * dprobs, axis=-1, keepdims=True)
    dscores = (probs * (dprobs - delta)).astype(jnp.bfloat16)
    query_grads = (
        jnp.einsum("grk,kd->rgd", dscores, key_part, preferred_element_type=jnp.float32)
        * softmax_scale
    )
    key_gradient_rows = (
        jnp.einsum("grk,rgd->kd", dscores, query_part, preferred_element_type=jnp.float32)
        * softmax_scale
    )
    return (query_grads, key_gradient_rows, value_gradient_rows)


def block_grads(query_rows, grad_rows, key_window, value_window, allowed):
    row_count, head_count, width = query_rows.shape
    group_count = key_window.shape[1]
    heads_per_group = head_count // group_count
    query_split = query_rows.reshape(row_count, group_count, heads_per_group, width).transpose(
        1, 0, 2, 3
    )
    grad_split = grad_rows.reshape(row_count, group_count, heads_per_group, width).transpose(
        1, 0, 2, 3
    )
    key_split = key_window.transpose(1, 0, 2)
    value_split = value_window.transpose(1, 0, 2)
    query_grads, key_gradient_rows, value_gradient_rows = lax.map(
        lambda packed: head_grads(packed[0], packed[1], packed[2], packed[3], allowed),
        (query_split, grad_split, key_split, value_split),
    )
    query_grads = query_grads.transpose(1, 0, 2, 3).reshape(row_count, head_count, width)
    return (
        query_grads,
        key_gradient_rows.transpose(1, 0, 2),
        value_gradient_rows.transpose(1, 0, 2),
    )


def shards(queries, key_vector_rows, value_vector_rows, grad_out):
    tok_rows = key_vector_rows.shape[0]
    block_index = lax.axis_index(("inner", "outer"))
    query_rows, grad_rows = (
        lax.all_to_all(queries, "head", split_axis=1, concat_axis=0, tiled=True),
        lax.all_to_all(grad_out, "head", split_axis=1, concat_axis=0, tiled=True),
    )
    source = (key_vector_rows, value_vector_rows)
    query_positions = block_index * tok_rows + jnp.arange(tok_rows, dtype=jnp.int32)
    arrived = []
    for shift_by in (2, 1):
        arrived.append(from_behind((source[0], source[1]), ("inner", "outer"), shift_by))
    key_window = jnp.concatenate([arrived[0][0], arrived[1][0], source[0]], axis=0)
    value_window = jnp.concatenate([arrived[0][1], arrived[1][1], source[1]], axis=0)
    key_positions = (block_index - 2) * tok_rows + jnp.arange(3 * tok_rows, dtype=jnp.int32)
    allowed = (key_positions[None, :] <= query_positions[:, None]) & (key_positions[None, :] >= 0)
    query_grads, key_gradient_rows, value_gradient_rows = block_grads(
        query_rows, grad_rows, key_window, value_window, allowed
    )
    query_result = lax.all_to_all(
        query_grads.astype(jnp.bfloat16), "head", split_axis=0, concat_axis=1, tiled=True
    )
    key_slot_rows = key_gradient_rows.reshape(
        3, tok_rows, key_gradient_rows.shape[1], key_gradient_rows.shape[2]
    )
    value_slot_rows = value_gradient_rows.reshape(
        3, tok_rows, value_gradient_rows.shape[1], value_gradient_rows.shape[2]
    )
    key_total = key_slot_rows[2]
    value_total = value_slot_rows[2]
    for back_by in (1, 2):
        key_back, value_back = from_behind(
            (key_slot_rows[2 - back_by], value_slot_rows[2 - back_by]), ("inner", "outer"), -back_by
        )
        key_total = key_total + key_back
        value_total = value_total + value_back
    return (query_result, key_total.astype(jnp.bfloat16), value_total.astype(jnp.bfloat16))


def solution(mesh):
    return jax.shard_map(
        shards,
        mesh=mesh,
        in_specs=(
            P(("inner", "outer", "head"), None, None),
            P(("inner", "outer"), "head", None),
            P(("inner", "outer"), "head", None),
            P(("inner", "outer", "head"), None, None),
        ),
        out_specs=(
            P(("inner", "outer", "head"), None, None),
            P(("inner", "outer"), "head", None),
            P(("inner", "outer"), "head", None),
        ),
        check_vma=False,
    )
```

profile of v0, /device:TPU:0, one launch (start us, length us, event | category | flops | bytes accessed | tf_op | source)
XLA Modules:
  0.0 182.1 jit_solution(10710460803360977241)
XLA Ops:
  0.7 2.9 %copy.51 = bf16[64,64,128]{2,0,1:T(8,128)(2,1)} copy(bf16[64,64,128]{2,1,0:T(8,128)(2,1)} %param.6) | data formatting | bytes 2097152 | tf_op args[0]
  3.6 4.2 %all-to-all-start = ((bf16[64,64,128]{2,0,1:T(8,128)(2,1)}), bf16[64,64,128]{2,0,1:T(8,128)(2,1)S(1)}, u32[]{:S(2)}, u32[]{:S(2)}) async-start(bf16[64,64,128]{2,0,1:T(8,128)(2,1)} %copy.51), calls=%async_computation | async-start | bytes 2097152 | tf_op jit(solution)/shard_map/all_to_all | solution.py:69
  7.8 2.9 %copy.56 = bf16[64,64,128]{2,0,1:T(8,128)(2,1)} copy(bf16[64,64,128]{2,1,0:T(8,128)(2,1)} %param.9) | data formatting | bytes 2097152 | tf_op args[3]
  10.7 11.5 %all-to-all-done = bf16[64,64,128]{2,0,1:T(8,128)(2,1)S(1)} async-done(((bf16[64,64,128]{2,0,1:T(8,128)(2,1)}), bf16[64,64,128]{2,0,1:T(8,128)(2,1)S(1)}, u32[]{:S(2)}, u32[]{:S(2)}) %all-to-all-start) | async-done | bytes 1048608 | tf_op jit(solution)/shard_map/all_to_all | solution.py:69
  22.2 3.5 %all-to-all-start.1 = ((bf16[64,64,128]{2,0,1:T(8,128)(2,1)}), bf16[64,64,128]{2,0,1:T(8,128)(2,1)S(1)}, u32[]{:S(2)}, u32[]{:S(2)}) async-start(bf16[64,64,128]{2,0,1:T(8,128)(2,1)} %copy.56), calls=%async_computation.1 | async-start | bytes 2097152 | tf_op jit(solution)/shard_map/all_to_all | solution.py:70
  25.8 5.2 %collective-permute-start = (bf16[256,2,128]{2,0,1:T(8,128)(2,1)S(1)}, bf16[256,2,128]{2,0,1:T(8,128)(2,1)S(1)}, u32[]{:S(2)}, u32[]{:S(2)}) collective-permute-start(bf16[256,2,128]{2,0,1:T(8,128)(2,1)S(1)} %copy.48), channel_id=1, source_target_pairs={{0,8},{4,12},{8,16},{12,20},{16,24},{20,28},{1,9},{5,13},{9,17},{1... | collective-permute-start | bytes 393224 | tf_op jit(solution)/shard_map/ppermute | solution.py:10
  31.0 3.5 %collective-permute-start.1 = (bf16[256,2,128]{2,0,1:T(8,128)(2,1)S(1)}, bf16[256,2,128]{2,0,1:T(8,128)(2,1)S(1)}, u32[]{:S(2)}, u32[]{:S(2)}) collective-permute-start(bf16[256,2,128]{2,0,1:T(8,128)(2,1)S(1)} %copy.48), channel_id=1, source_target_pairs={{0,4},{4,8},{8,12},{12,16},{16,20},{20,24},{24,28},{1,5},{5,9},{9,... | collective-permute-start | bytes 393224 | tf_op jit(solution)/shard_map/ppermute | solution.py:10
  34.6 3.2 %collective-permute-start.2 = (bf16[256,2,128]{2,0,1:T(8,128)(2,1)S(1)}, bf16[256,2,128]{2,0,1:T(8,128)(2,1)S(1)}, u32[]{:S(2)}, u32[]{:S(2)}) collective-permute-start(bf16[256,2,128]{2,0,1:T(8,128)(2,1)S(1)} %copy.53), channel_id=1, source_target_pairs={{0,8},{4,12},{8,16},{12,20},{16,24},{20,28},{1,9},{5,13},{9,17},{1... | collective-permute-start | bytes 393224 | tf_op jit(solution)/shard_map/ppermute | solution.py:10
  37.8 4.4 %collective-permute-start.3 = (bf16[256,2,128]{2,0,1:T(8,128)(2,1)S(1)}, bf16[256,2,128]{2,0,1:T(8,128)(2,1)S(1)}, u32[]{:S(2)}, u32[]{:S(2)}) collective-permute-start(bf16[256,2,128]{2,0,1:T(8,128)(2,1)S(1)} %copy.53), channel_id=1, source_target_pairs={{0,4},{4,8},{8,12},{12,16},{16,20},{20,24},{24,28},{1,5},{5,9},{9,... | collective-permute-start | bytes 393224 | tf_op jit(solution)/shard_map/ppermute | solution.py:10
  45.9 81.8 %while.15 = (s32[]{:T(128)}, bf16[2,256,8,128]{1,3,2,0:T(8,128)(2,1)}, f32[2,768,128]{2,0,1:T(2,128)}, f32[2,768,128]{2,0,1:T(2,128)}, bf16[2,768,128]{2,1,0:T(8...) while((s32[]{:T(128)}, ...), condition=%wide.region_4.5_spmd.clone, body=%wide.region_0.4_spmd.clone.sunk | while | flops 2034465536 | bytes 100918376 | solution.py:53
  47.0 5.7 %fusion.96 = (f32[8,256]{1,0:T(8,128)S(1)}, f32[8,256,768]{1,2,0:T(8,128)}) fusion(pred[256,768]{0,1:T(8,128)(4,1)S(1)} %compare_and_fusion.2, bf16[2,256,8,128]{3,1,2,0:T(8,128)(2,1)S(1)} %get-tuple-element.218, s32[]{:T(128)} %get-tuple-element.200, bf16[2,768,128]{2,1,0:T(8,128)(2,1)} %get-tuple-element.217), kind=kOutput, calls=%fused_computation.63.clone.1 | convolution fusion | flops 408945408 | bytes 7218176 | tf_op jit(solution)/shard_map/while/body/eval_jaxpr/sub | solution.py:21
  52.6 3.9 %fusion.97 = (f32[8,256]{1,0:T(8,128)S(1)}, f32[768,256,8]{1,0,2:T(8,128)S(1)}) fusion(f32[8,256,768]{1,2,0:T(8,128)} %get-tuple-element.183, f32[8,256]{1,0:T(8,128)S(1)} %get-tuple-element.184, bf16[2,256,8,128]{3,1,2,0:T(8,128)(2,1)S(1)} %copy-done.3, s32[]{:T(128)} %get-tuple-element.200, bf16[2,768,128]{2,1,0:T(8,128)(2,1)S(1)} %get-tuple-element.219), kind=kOutput, calls=%fused_computation.4.clone.1 | convolution fusion | flops 407369728 | bytes 13321216 | tf_op jit(solution)/shard_map/while/body/eval_jaxpr/rgd,kd->grk/dot_general | solution.py:27
  60.4 10.6 %dynamic_update_slice.19 = f32[2,768,128]{2,0,1:T(2,128)} dynamic-update-slice(f32[2,768,128]{2,0,1:T(2,128)} %get-tuple-element.202, f32[1,768,128]{2,0,1:T(1,128)S(1)} %bitcast.141, s32[]{:T(128)} %get-tuple-element.200, s32[]{:T(128)} %constant.13.clone.1..sunk, s32[]{:T(128)} %constant.13.clone.1..sunk) | dynamic-update-slice | bytes 786436 | tf_op jit(solution)/shard_map/while/body/jit(dynamic_update_index_in_dim)/dynamic_update_slice | solution.py:53
  73.3 4.0 %fusion.101 = f32[768,128,1]{1,0,2:T(8,128)S(1)} fusion(bf16[2,256,8,128]{3,1,2,0:T(8,128)(2,1)} %get-tuple-element.220, s32[]{:T(128)} %get-tuple-element.200, f32[8,256,768]{1,2,0:T(8,128)} %get-tuple-element.183, f32[8,256]{1,0:T(8,128)S(1)} %get-tuple-element.184), kind=kOutput, calls=%fused_computation.10.clone.1 | convolution fusion | flops 405798912 | bytes 7217664 | tf_op jit(solution)/shard_map/while/body/eval_jaxpr/grk,rgd->kd/dot_general | solution.py:24
  77.3 8.6 %dynamic_update_slice.20 = f32[2,768,128]{2,0,1:T(2,128)S(1)} dynamic-update-slice(f32[2,768,128]{2,0,1:T(2,128)S(1)} %copy-done.4, f32[1,768,128]{2,0,1:T(1,128)S(1)} %bitcast.143, s32[]{:T(128)} %get-tuple-element.200, s32[]{:T(128)} %constant.13.clone.1..sunk, s32[]{:T(128)} %constant.13.clone.1..sunk) | dynamic-update-slice | bytes 786436 | tf_op jit(solution)/shard_map/while/body/jit(dynamic_update_index_in_dim)/dynamic_update_slice | solution.py:53
  87.9 5.7 %fusion.96 = (f32[8,256]{1,0:T(8,128)S(1)}, f32[8,256,768]{1,2,0:T(8,128)}) fusion(pred[256,768]{0,1:T(8,128)(4,1)S(1)} %compare_and_fusion.2, bf16[2,256,8,128]{3,1,2,0:T(8,128)(2,1)S(1)} %get-tuple-element.218, s32[]{:T(128)} %get-tuple-element.200, bf16[2,768,128]{2,1,0:T(8,128)(2,1)} %get-tuple-element.217), kind=kOutput, calls=%fused_computation.63.clone.1 | convolution fusion | flops 408945408 | bytes 7218176 | tf_op jit(solution)/shard_map/while/body/eval_jaxpr/sub | solution.py:21
  93.5 3.9 %fusion.97 = (f32[8,256]{1,0:T(8,128)S(1)}, f32[768,256,8]{1,0,2:T(8,128)S(1)}) fusion(f32[8,256,768]{1,2,0:T(8,128)} %get-tuple-element.183, f32[8,256]{1,0:T(8,128)S(1)} %get-tuple-element.184, bf16[2,256,8,128]{3,1,2,0:T(8,128)(2,1)S(1)} %copy-done.3, s32[]{:T(128)} %get-tuple-element.200, bf16[2,768,128]{2,1,0:T(8,128)(2,1)S(1)} %get-tuple-element.219), kind=kOutput, calls=%fused_computation.4.clone.1 | convolution fusion | flops 407369728 | bytes 13321216 | tf_op jit(solution)/shard_map/while/body/eval_jaxpr/rgd,kd->grk/dot_general | solution.py:27
  101.3 10.6 %dynamic_update_slice.19 = f32[2,768,128]{2,0,1:T(2,128)} dynamic-update-slice(f32[2,768,128]{2,0,1:T(2,128)} %get-tuple-element.202, f32[1,768,128]{2,0,1:T(1,128)S(1)} %bitcast.141, s32[]{:T(128)} %get-tuple-element.200, s32[]{:T(128)} %constant.13.clone.1..sunk, s32[]{:T(128)} %constant.13.clone.1..sunk) | dynamic-update-slice | bytes 786436 | tf_op jit(solution)/shard_map/while/body/jit(dynamic_update_index_in_dim)/dynamic_update_slice | solution.py:53
  114.2 4.0 %fusion.101 = f32[768,128,1]{1,0,2:T(8,128)S(1)} fusion(bf16[2,256,8,128]{3,1,2,0:T(8,128)(2,1)} %get-tuple-element.220, s32[]{:T(128)} %get-tuple-element.200, f32[8,256,768]{1,2,0:T(8,128)} %get-tuple-element.183, f32[8,256]{1,0:T(8,128)S(1)} %get-tuple-element.184), kind=kOutput, calls=%fused_computation.10.clone.1 | convolution fusion | flops 405798912 | bytes 7217664 | tf_op jit(solution)/shard_map/while/body/eval_jaxpr/grk,rgd->kd/dot_general | solution.py:24
  118.2 8.6 %dynamic_update_slice.20 = f32[2,768,128]{2,0,1:T(2,128)S(1)} dynamic-update-slice(f32[2,768,128]{2,0,1:T(2,128)S(1)} %copy-done.4, f32[1,768,128]{2,0,1:T(1,128)S(1)} %bitcast.143, s32[]{:T(128)} %get-tuple-element.200, s32[]{:T(128)} %constant.13.clone.1..sunk, s32[]{:T(128)} %constant.13.clone.1..sunk) | dynamic-update-slice | bytes 786436 | tf_op jit(solution)/shard_map/while/body/jit(dynamic_update_index_in_dim)/dynamic_update_slice | solution.py:53
  130.3 3.5 %all-to-all-start.2 = ((bf16[256,16,128]{2,1,0:T(8,128)(2,1)}), bf16[256,16,128]{2,1,0:T(8,128)(2,1)S(1)}, u32[]{:S(2)}, u32[]{:S(2)}) async-start(bf16[256,16,128]{2,1,0:T(8,128)(2,1)} %bitcast.11), calls=%async_computation.2 | async-start | bytes 2097152 | tf_op jit(solution)/shard_map/all_to_all | solution.py:84
  141.1 8.1 %collective-permute-done.6 = f32[256,2,128]{2,1,0:T(2,128)S(1)} collective-permute-done((f32[256,2,128]{2,1,0:T(2,128)S(1)}, f32[256,2,128]{2,1,0:T(2,128)S(1)}, u32[]{:S(2)}, u32[]{:S(2)}) %collective-permute-start.6) | collective-permute-done | bytes 262176 | tf_op jit(solution)/shard_map/ppermute | solution.py:10
  149.2 13.1 %collective-permute-done.7 = f32[256,2,128]{2,1,0:T(2,128)S(1)} collective-permute-done((f32[256,2,128]{2,1,0:T(2,128)S(1)}, f32[256,2,128]{2,1,0:T(2,128)S(1)}, u32[]{:S(2)}, u32[]{:S(2)}) %collective-permute-start.7) | collective-permute-done | bytes 262176 | tf_op jit(solution)/shard_map/ppermute | solution.py:10
  164.1 14.8 %collective-permute-done.5 = f32[256,2,128]{2,1,0:T(2,128)S(1)} collective-permute-done((f32[256,2,128]{2,1,0:T(2,128)S(1)}, f32[256,2,128]{2,1,0:T(2,128)S(1)}, u32[]{:S(2)}, u32[]{:S(2)}) %collective-permute-start.5) | collective-permute-done | bytes 262176 | tf_op jit(solution)/shard_map/ppermute | solution.py:10
  (73 shorter events, 34.8 us)
Async XLA Ops:
  0.6 25.1 %copy-start.8 = (bf16[256,2,128]{2,1,0:T(2,128)(2,1)S(1)}, bf16[256,2,128]{2,1,0:T(2,128)(2,1)}, u32[]{:S(2)}) copy-start(bf16[256,2,128]{2,1,0:T(2,128)(2,1)} %param.7) | copy-start | bytes 393220
  0.6 33.9 %copy-start.9 = (bf16[256,2,128]{2,1,0:T(2,128)(2,1)S(1)}, bf16[256,2,128]{2,1,0:T(2,128)(2,1)}, u32[]{:S(2)}) copy-start(bf16[256,2,128]{2,1,0:T(2,128)(2,1)} %param.8) | copy-start | bytes 393220
  3.6 18.7 %all-to-all-start = ((bf16[64,64,128]{2,0,1:T(8,128)(2,1)}), bf16[64,64,128]{2,0,1:T(8,128)(2,1)S(1)}, u32[]{:S(2)}, u32[]{:S(2)}) async-start(bf16[64,64,128]{2,0,1:T(8,128)(2,1)} %copy.51), calls=%async_computation | async-start | bytes 2097152 | tf_op jit(solution)/shard_map/all_to_all | solution.py:69
  22.2 22.6 %all-to-all-start.1 = ((bf16[64,64,128]{2,0,1:T(8,128)(2,1)}), bf16[64,64,128]{2,0,1:T(8,128)(2,1)S(1)}, u32[]{:S(2)}, u32[]{:S(2)}) async-start(bf16[64,64,128]{2,0,1:T(8,128)(2,1)} %copy.56), calls=%async_computation.1 | async-start | bytes 2097152 | tf_op jit(solution)/shard_map/all_to_all | solution.py:70
  25.8 17.0 %collective-permute-start = (bf16[256,2,128]{2,0,1:T(8,128)(2,1)S(1)}, bf16[256,2,128]{2,0,1:T(8,128)(2,1)S(1)}, u32[]{:S(2)}, u32[]{:S(2)}) collective-permute-start(bf16[256,2,128]{2,0,1:T(8,128)(2,1)S(1)} %copy.48), channel_id=1, source_target_pairs={{0,8},{4,12},{8,16},{12,20},{16,24},{20,28},{1,9},{5,13},{9,17},{1... | collective-permute-start | bytes 393224 | tf_op jit(solution)/shard_map/ppermute | solution.py:10
  31.0 11.7 %collective-permute-start.1 = (bf16[256,2,128]{2,0,1:T(8,128)(2,1)S(1)}, bf16[256,2,128]{2,0,1:T(8,128)(2,1)S(1)}, u32[]{:S(2)}, u32[]{:S(2)}) collective-permute-start(bf16[256,2,128]{2,0,1:T(8,128)(2,1)S(1)} %copy.48), channel_id=1, source_target_pairs={{0,4},{4,8},{8,12},{12,16},{16,20},{20,24},{24,28},{1,5},{5,9},{9,... | collective-permute-start | bytes 393224 | tf_op jit(solution)/shard_map/ppermute | solution.py:10
  34.6 9.0 %collective-permute-start.2 = (bf16[256,2,128]{2,0,1:T(8,128)(2,1)S(1)}, bf16[256,2,128]{2,0,1:T(8,128)(2,1)S(1)}, u32[]{:S(2)}, u32[]{:S(2)}) collective-permute-start(bf16[256,2,128]{2,0,1:T(8,128)(2,1)S(1)} %copy.53), channel_id=1, source_target_pairs={{0,8},{4,12},{8,16},{12,20},{16,24},{20,28},{1,9},{5,13},{9,17},{1... | collective-permute-start | bytes 393224 | tf_op jit(solution)/shard_map/ppermute | solution.py:10
  37.8 6.9 %collective-permute-start.3 = (bf16[256,2,128]{2,0,1:T(8,128)(2,1)S(1)}, bf16[256,2,128]{2,0,1:T(8,128)(2,1)S(1)}, u32[]{:S(2)}, u32[]{:S(2)}) collective-permute-start(bf16[256,2,128]{2,0,1:T(8,128)(2,1)S(1)} %copy.53), channel_id=1, source_target_pairs={{0,4},{4,8},{8,12},{12,16},{16,20},{20,24},{24,28},{1,5},{5,9},{9,... | collective-permute-start | bytes 393224 | tf_op jit(solution)/shard_map/ppermute | solution.py:10
  45.9 10.7 %copy-start.1 = (bf16[2,256,8,128]{3,1,2,0:T(8,128)(2,1)}, bf16[2,256,8,128]{3,1,2,0:T(8,128)(2,1)S(1)}, u32[]{:S(2)}) copy-start(bf16[2,256,8,128]{3,1,2,0:T(8,128)(2,1)S(1)} %get-tuple-element.218) | copy-start | bytes 3145732 | tf_op jit(solution)/shard_map/while
  45.9 10.7 %copy-start.6 = (bf16[2,768,128]{2,1,0:T(8,128)(2,1)}, bf16[2,768,128]{2,1,0:T(8,128)(2,1)S(1)}, u32[]{:S(2)}) copy-start(bf16[2,768,128]{2,1,0:T(8,128)(2,1)S(1)} %get-tuple-element.219) | copy-start | bytes 1179652 | tf_op jit(solution)/shard_map/while
  45.9 6.7 %copy-start.3 = (bf16[2,256,8,128]{3,1,2,0:T(8,128)(2,1)S(1)}, bf16[2,256,8,128]{3,1,2,0:T(8,128)(2,1)}, u32[]{:S(2)}) copy-start(bf16[2,256,8,128]{3,1,2,0:T(8,128)(2,1)} %get-tuple-element.220) | copy-start | bytes 3145732 | tf_op jit(solution)/shard_map/while
  52.6 4.6 %copy-start = (f32[8,256,768]{1,2,0:T(8,128)S(1)}, f32[8,256,768]{1,2,0:T(8,128)}, u32[]{:S(2)}) copy-start(f32[8,256,768]{1,2,0:T(8,128)} %get-tuple-element.183) | copy-start | bytes 18874372 | tf_op jit(solution)/shard_map/while
  73.3 13.4 %copy-start.2 = (bf16[2,256,8,128]{3,1,2,0:T(8,128)(2,1)S(1)}, bf16[2,256,8,128]{3,1,2,0:T(8,128)(2,1)}, u32[]{:S(2)}) copy-start(bf16[2,256,8,128]{3,1,2,0:T(8,128)(2,1)} %copy-done.1) | copy-start | bytes 3145732 | tf_op jit(solution)/shard_map/while
  73.3 13.4 %copy-start.7 = (bf16[2,768,128]{2,1,0:T(8,128)(2,1)S(1)}, bf16[2,768,128]{2,1,0:T(8,128)(2,1)}, u32[]{:S(2)}) copy-start(bf16[2,768,128]{2,1,0:T(8,128)(2,1)} %copy-done.6) | copy-start | bytes 1179652 | tf_op jit(solution)/shard_map/while
  86.8 10.7 %copy-start.1 = (bf16[2,256,8,128]{3,1,2,0:T(8,128)(2,1)}, bf16[2,256,8,128]{3,1,2,0:T(8,128)(2,1)S(1)}, u32[]{:S(2)}) copy-start(bf16[2,256,8,128]{3,1,2,0:T(8,128)(2,1)S(1)} %get-tuple-element.218) | copy-start | bytes 3145732 | tf_op jit(solution)/shard_map/while
  86.8 10.7 %copy-start.6 = (bf16[2,768,128]{2,1,0:T(8,128)(2,1)}, bf16[2,768,128]{2,1,0:T(8,128)(2,1)S(1)}, u32[]{:S(2)}) copy-start(bf16[2,768,128]{2,1,0:T(8,128)(2,1)S(1)} %get-tuple-element.219) | copy-start | bytes 1179652 | tf_op jit(solution)/shard_map/while
  86.8 6.7 %copy-start.3 = (bf16[2,256,8,128]{3,1,2,0:T(8,128)(2,1)S(1)}, bf16[2,256,8,128]{3,1,2,0:T(8,128)(2,1)}, u32[]{:S(2)}) copy-start(bf16[2,256,8,128]{3,1,2,0:T(8,128)(2,1)} %get-tuple-element.220) | copy-start | bytes 3145732 | tf_op jit(solution)/shard_map/while
  114.2 13.4 %copy-start.2 = (bf16[2,256,8,128]{3,1,2,0:T(8,128)(2,1)S(1)}, bf16[2,256,8,128]{3,1,2,0:T(8,128)(2,1)}, u32[]{:S(2)}) copy-start(bf16[2,256,8,128]{3,1,2,0:T(8,128)(2,1)} %copy-done.1) | copy-start | bytes 3145732 | tf_op jit(solution)/shard_map/while
  114.2 13.4 %copy-start.7 = (bf16[2,768,128]{2,1,0:T(8,128)(2,1)S(1)}, bf16[2,768,128]{2,1,0:T(8,128)(2,1)}, u32[]{:S(2)}) copy-start(bf16[2,768,128]{2,1,0:T(8,128)(2,1)} %copy-done.6) | copy-start | bytes 1179652 | tf_op jit(solution)/shard_map/while
  130.3 50.5 %all-to-all-start.2 = ((bf16[256,16,128]{2,1,0:T(8,128)(2,1)}), bf16[256,16,128]{2,1,0:T(8,128)(2,1)S(1)}, u32[]{:S(2)}, u32[]{:S(2)}) async-start(bf16[256,16,128]{2,1,0:T(8,128)(2,1)} %bitcast.11), calls=%async_computation.2 | async-start | bytes 2097152 | tf_op jit(solution)/shard_map/all_to_all | solution.py:84
  134.9 14.3 %collective-permute-start.6 = (f32[256,2,128]{2,1,0:T(2,128)S(1)}, f32[256,2,128]{2,1,0:T(2,128)S(1)}, u32[]{:S(2)}, u32[]{:S(2)}) collective-permute-start(f32[256,2,128]{2,1,0:T(2,128)S(1)} %get-tuple-element.108), channel_id=1, source_target_pairs={{4,0},{8,4},{12,8},{16,12},{20,16},{24,20},{28,24},{5,1},{9,5},{13... | collective-permute-start | bytes 786440 | tf_op jit(solution)/shard_map/ppermute | solution.py:10
  136.2 26.2 %collective-permute-start.7 = (f32[256,2,128]{2,1,0:T(2,128)S(1)}, f32[256,2,128]{2,1,0:T(2,128)S(1)}, u32[]{:S(2)}, u32[]{:S(2)}) collective-permute-start(f32[256,2,128]{2,1,0:T(2,128)S(1)} %get-tuple-element.109), channel_id=1, source_target_pairs={{8,0},{12,4},{16,8},{20,12},{24,16},{28,20},{9,1},{13,5},{17,9},{2... | collective-permute-start | bytes 786440 | tf_op jit(solution)/shard_map/ppermute | solution.py:10
  138.5 25.6 %collective-permute-start.4 = (f32[256,2,128]{2,1,0:T(2,128)S(1)}, f32[256,2,128]{2,1,0:T(2,128)S(1)}, u32[]{:S(2)}, u32[]{:S(2)}) collective-permute-start(f32[256,2,128]{2,1,0:T(2,128)S(1)} %get-tuple-element.110), channel_id=1, source_target_pairs={{4,0},{8,4},{12,8},{16,12},{20,16},{24,20},{28,24},{5,1},{9,5},{13... | collective-permute-start | bytes 786440 | tf_op jit(solution)/shard_map/ppermute | solution.py:10
  139.8 39.1 %collective-permute-start.5 = (f32[256,2,128]{2,1,0:T(2,128)S(1)}, f32[256,2,128]{2,1,0:T(2,128)S(1)}, u32[]{:S(2)}, u32[]{:S(2)}) collective-permute-start(f32[256,2,128]{2,1,0:T(2,128)S(1)} %get-tuple-element.111), channel_id=1, source_target_pairs={{8,0},{12,4},{16,8},{20,12},{24,16},{28,20},{9,1},{13,5},{17,9},{2... | collective-permute-start | bytes 786440 | tf_op jit(solution)/shard_map/ppermute | solution.py:10
  (5 other events, 14.3 us)
where the time goes:
time: 184 us; the launch traced here: 182 us
  local copies, waits for them, and re-layouts  54.4 us (30%)
  waiting for transfers between devices  48.7 us (26%)
  matrix products  35.8 us (19%)
  starting transfers between devices  32.7 us (18%)
  other arithmetic  9.45 us (5%)
    dynamic_update_slice x4, local copies, waits for them, and re-layouts, block_grads(): lax.map(lambda packed: head_grads(packed[0], packed[1], packed[2], packed...  38.2 us
    ppermute x8, waiting for transfers between devices, from_behind(): return lax.ppermute(value, axis, pairs)  37.1 us
    ppermute x8, starting transfers between devices, from_behind(): return lax.ppermute(value, axis, pairs)  21.5 us
    all_to_all x1, waiting for transfers between devices, shards(): lax.all_to_all(queries, 'head', split_axis=1, concat_axis=0, tiled=True)  11.5 us
    sub x2, matrix products, head_grads(): probs = jnp.exp(scores - highest)  11.3 us
    dot_general x2, matrix products, head_grads(): jnp.einsum('grk,rgd->kd', probs_low, grad_part, preferred_element_type=jn...  7.94 us
    dot_general x2, matrix products, head_grads(): jnp.einsum('rgd,kd->grk', grad_part, value_part, preferred_element_type=j...  7.84 us
    unnamed x8, local copies, waits for them, and re-layouts  5.86 us
  transfers between devices with their start and end apart: 11, of which 5 were waited for; matrix products, arithmetic and copies ran while one was open for 6% of the time, Pallas kernels for 0%

commit v1 on v0

--- a/solution.py
+++ b/solution.py
@@ -66,7 +66,12 @@
     tok_rows = key_vector_rows.shape[0]
     block_index = lax.axis_index(("inner", "outer"))
     query_rows, grad_rows = (
-        lax.all_to_all(queries, "head", split_axis=1, concat_axis=0, tiled=True),
+        jnp.concatenate(
+            lax.all_to_all(
+                jnp.stack(jnp.split(queries, lax.axis_size("head"), axis=1)), "head", 0, 0
+            ),
+            axis=0,
+        ),
         lax.all_to_all(grad_out, "head", split_axis=1, concat_axis=0, tiled=True),
     )
     source = (key_vector_rows, value_vector_rows)

time: 184 us -> 184 us (level)
  local copies, waits for them, and re-layouts: 54.4 us -> 52 us
    all_to_all x1, waiting for transfers between devices: 0.01 us -> 11.9 us  [shards(): lax.all_to_all(grad_out, 'head', split_axis=1, concat_axis=0, tiled=True)]
    all_to_all x1, waiting for transfers between devices: 11.5 us -> 0.01 us  [shards(): lax.all_to_all(jnp.stack(jnp.split(queries, lax.axis_size('head'), axis=1...]
    unnamed x8 -> x7, local copies, waits for them, and re-layouts: 5.86 us -> 2.96 us
where the time goes in v1:
time: 184 us; the launch traced here: 182 us
  local copies, waits for them, and re-layouts  52 us (28%)
  waiting for transfers between devices  49.1 us (27%)
  matrix products  36 us (20%)
  starting transfers between devices  32.7 us (18%)
  other arithmetic  11.2 us (6%)
    dynamic_update_slice x4, local copies, waits for them, and re-layouts, block_grads(): lax.map(lambda packed: head_grads(packed[0], packed[1], packed[2], packed...  38.2 us
    ppermute x8, waiting for transfers between devices, from_behind(): return lax.ppermute(value, axis, pairs)  37.2 us
    ppermute x8, starting transfers between devices, from_behind(): return lax.ppermute(value, axis, pairs)  21.5 us
    all_to_all x1, waiting for transfers between devices, shards(): lax.all_to_all(grad_out, 'head', split_axis=1, concat_axis=0, tiled=True)  11.9 us
    sub x2, matrix products, head_grads(): probs = jnp.exp(scores - highest)  11.3 us
    dot_general x2, matrix products, head_grads(): jnp.einsum('rgd,kd->grk', grad_part, value_part, preferred_element_type=j...  8.04 us
    dot_general x2, matrix products, head_grads(): jnp.einsum('grk,rgd->kd', probs_low, grad_part, preferred_element_type=jn...  7.95 us
    dot_general x2, matrix products, head_grads(): jnp.einsum('grk,kd->rgd', dscores, key_part, preferred_element_type=jnp.f...  4.66 us
  transfers between devices with their start and end apart: 11, of which 5 were waited for; matrix products, arithmetic and copies ran while one was open for 6% of the time, Pallas kernels for 0%

profile of v1, /device:TPU:0, one launch (start us, length us, event | category | flops | bytes accessed | tf_op | source)
XLA Modules:
  0.0 182.1 jit_solution(11861679983969731441)
XLA Ops:
  0.7 2.9 %copy.55 = bf16[64,64,128]{2,0,1:T(8,128)(2,1)} copy(bf16[64,64,128]{2,1,0:T(8,128)(2,1)} %param.9) | data formatting | bytes 2097152 | tf_op args[3]
  3.6 4.2 %all-to-all-start.1 = ((bf16[64,64,128]{2,0,1:T(8,128)(2,1)}), bf16[64,64,128]{2,0,1:T(8,128)(2,1)S(1)}, u32[]{:S(2)}, u32[]{:S(2)}) async-start(bf16[64,64,128]{2,0,1:T(8,128)(2,1)} %copy.55), calls=%async_computation.1 | async-start | bytes 2097152 | tf_op jit(solution)/shard_map/all_to_all | solution.py:75
  10.3 11.9 %all-to-all-done.1 = bf16[64,64,128]{2,0,1:T(8,128)(2,1)S(1)} async-done(((bf16[64,64,128]{2,0,1:T(8,128)(2,1)}), bf16[64,64,128]{2,0,1:T(8,128)(2,1)S(1)}, u32[]{:S(2)}, u32[]{:S(2)}) %all-to-all-start.1) | async-done | bytes 1048608 | tf_op jit(solution)/shard_map/all_to_all | solution.py:75
  22.2 3.5 %all-to-all-start = ((bf16[4,64,16,128]{3,2,1,0:T(8,128)(2,1)}), bf16[4,64,16,128]{3,2,1,0:T(8,128)(2,1)S(1)}, u32[]{:S(2)}, u32[]{:S(2)}) async-start(bf16[4,64,16,128]{3,2,1,0:T(8,128)(2,1)} %pad_maximum_fusion), calls=%async_computation | async-start | bytes 2097152 | tf_op jit(solution)/shard_map/all_to_all | solution.py:70
  25.8 5.2 %collective-permute-start = (bf16[256,2,128]{2,0,1:T(8,128)(2,1)S(1)}, bf16[256,2,128]{2,0,1:T(8,128)(2,1)S(1)}, u32[]{:S(2)}, u32[]{:S(2)}) collective-permute-start(bf16[256,2,128]{2,0,1:T(8,128)(2,1)S(1)} %copy.48), channel_id=1, source_target_pairs={{0,8},{4,12},{8,16},{12,20},{16,24},{20,28},{1,9},{5,13},{9,17},{1... | collective-permute-start | bytes 393224 | tf_op jit(solution)/shard_map/ppermute | solution.py:10
  31.0 3.5 %collective-permute-start.1 = (bf16[256,2,128]{2,0,1:T(8,128)(2,1)S(1)}, bf16[256,2,128]{2,0,1:T(8,128)(2,1)S(1)}, u32[]{:S(2)}, u32[]{:S(2)}) collective-permute-start(bf16[256,2,128]{2,0,1:T(8,128)(2,1)S(1)} %copy.48), channel_id=1, source_target_pairs={{0,4},{4,8},{8,12},{12,16},{16,20},{20,24},{24,28},{1,5},{5,9},{9,... | collective-permute-start | bytes 393224 | tf_op jit(solution)/shard_map/ppermute | solution.py:10
  34.6 3.2 %collective-permute-start.2 = (bf16[256,2,128]{2,0,1:T(8,128)(2,1)S(1)}, bf16[256,2,128]{2,0,1:T(8,128)(2,1)S(1)}, u32[]{:S(2)}, u32[]{:S(2)}) collective-permute-start(bf16[256,2,128]{2,0,1:T(8,128)(2,1)S(1)} %copy.52), channel_id=1, source_target_pairs={{0,8},{4,12},{8,16},{12,20},{16,24},{20,28},{1,9},{5,13},{9,17},{1... | collective-permute-start | bytes 393224 | tf_op jit(solution)/shard_map/ppermute | solution.py:10
  37.8 4.4 %collective-permute-start.3 = (bf16[256,2,128]{2,0,1:T(8,128)(2,1)S(1)}, bf16[256,2,128]{2,0,1:T(8,128)(2,1)S(1)}, u32[]{:S(2)}, u32[]{:S(2)}) collective-permute-start(bf16[256,2,128]{2,0,1:T(8,128)(2,1)S(1)} %copy.52), channel_id=1, source_target_pairs={{0,4},{4,8},{8,12},{12,16},{16,20},{20,24},{24,28},{1,5},{5,9},{9,... | collective-permute-start | bytes 393224 | tf_op jit(solution)/shard_map/ppermute | solution.py:10
  45.8 81.8 %while.15 = (s32[]{:T(128)}, bf16[2,256,8,128]{1,3,2,0:T(8,128)(2,1)}, f32[2,768,128]{2,0,1:T(2,128)}, f32[2,768,128]{2,0,1:T(2,128)}, bf16[2,768,128]{2,1,0:T(8...) while((s32[]{:T(128)}, ...), condition=%wide.region_4.5_spmd.clone, body=%wide.region_0.4_spmd.clone.sunk | while | flops 2034465536 | bytes 101966936 | solution.py:53
  46.9 5.6 %fusion.96 = (f32[8,256]{1,0:T(8,128)S(1)}, f32[8,256,768]{1,2,0:T(8,128)}) fusion(pred[256,768]{0,1:T(8,128)(4,1)S(1)} %compare_and_fusion.2, bf16[2,256,8,128]{3,1,2,0:T(8,128)(2,1)S(1)} %get-tuple-element.222, s32[]{:T(128)} %get-tuple-element.204, bf16[2,768,128]{2,1,0:T(8,128)(2,1)} %get-tuple-element.221), kind=kOutput, calls=%fused_computation.68.clone.1 | convolution fusion | flops 408945408 | bytes 7218176 | tf_op jit(solution)/shard_map/while/body/eval_jaxpr/sub | solution.py:21
  52.5 4.0 %fusion.97 = (f32[8,256]{1,0:T(8,128)S(1)}, f32[768,256,8]{1,0,2:T(8,128)S(1)}) fusion(f32[8,256,768]{1,2,0:T(8,128)} %get-tuple-element.187, f32[8,256]{1,0:T(8,128)S(1)} %get-tuple-element.188, bf16[2,256,8,128]{3,1,2,0:T(8,128)(2,1)S(1)} %get-tuple-element.224, s32[]{:T(128)} %get-tuple-element.204, bf16[2,768,128]{2,1,0:T(8,128)(2,1)} %get-tuple-element.223), kind=kOutput, calls=%fused_computation.4.clone.1 | convolution fusion | flops 407369728 | bytes 13321216 | tf_op jit(solution)/shard_map/while/body/eval_jaxpr/rgd,kd->grk/dot_general | solution.py:27
  60.4 10.6 %dynamic_update_slice.19 = f32[2,768,128]{2,0,1:T(2,128)} dynamic-update-slice(f32[2,768,128]{2,0,1:T(2,128)} %get-tuple-element.206, f32[1,768,128]{2,0,1:T(1,128)S(1)} %bitcast.146, s32[]{:T(128)} %get-tuple-element.204, s32[]{:T(128)} %constant.13.clone.1..sunk, s32[]{:T(128)} %constant.13.clone.1..sunk) | dynamic-update-slice | bytes 786436 | tf_op jit(solution)/shard_map/while/body/jit(dynamic_update_index_in_dim)/dynamic_update_slice | solution.py:53
  73.3 4.0 %fusion.101 = f32[768,128,1]{1,0,2:T(8,128)S(1)} fusion(bf16[2,256,8,128]{3,1,2,0:T(8,128)(2,1)} %copy-done.3, s32[]{:T(128)} %get-tuple-element.204, f32[8,256,768]{1,2,0:T(8,128)} %get-tuple-element.187, f32[8,256]{1,0:T(8,128)S(1)} %get-tuple-element.188), kind=kOutput, calls=%fused_computation.10.clone.1 | convolution fusion | flops 405798912 | bytes 7217664 | tf_op jit(solution)/shard_map/while/body/eval_jaxpr/grk,rgd->kd/dot_general | solution.py:24
  77.3 8.6 %dynamic_update_slice.20 = f32[2,768,128]{2,0,1:T(2,128)S(1)} dynamic-update-slice(f32[2,768,128]{2,0,1:T(2,128)S(1)} %copy-done.5, f32[1,768,128]{2,0,1:T(1,128)S(1)} %bitcast.148, s32[]{:T(128)} %get-tuple-element.204, s32[]{:T(128)} %constant.13.clone.1..sunk, s32[]{:T(128)} %constant.13.clone.1..sunk) | dynamic-update-slice | bytes 786436 | tf_op jit(solution)/shard_map/while/body/jit(dynamic_update_index_in_dim)/dynamic_update_slice | solution.py:53
  87.8 5.7 %fusion.96 = (f32[8,256]{1,0:T(8,128)S(1)}, f32[8,256,768]{1,2,0:T(8,128)}) fusion(pred[256,768]{0,1:T(8,128)(4,1)S(1)} %compare_and_fusion.2, bf16[2,256,8,128]{3,1,2,0:T(8,128)(2,1)S(1)} %get-tuple-element.222, s32[]{:T(128)} %get-tuple-element.204, bf16[2,768,128]{2,1,0:T(8,128)(2,1)} %get-tuple-element.221), kind=kOutput, calls=%fused_computation.68.clone.1 | convolution fusion | flops 408945408 | bytes 7218176 | tf_op jit(solution)/shard_map/while/body/eval_jaxpr/sub | solution.py:21
  93.4 4.0 %fusion.97 = (f32[8,256]{1,0:T(8,128)S(1)}, f32[768,256,8]{1,0,2:T(8,128)S(1)}) fusion(f32[8,256,768]{1,2,0:T(8,128)} %get-tuple-element.187, f32[8,256]{1,0:T(8,128)S(1)} %get-tuple-element.188, bf16[2,256,8,128]{3,1,2,0:T(8,128)(2,1)S(1)} %get-tuple-element.224, s32[]{:T(128)} %get-tuple-element.204, bf16[2,768,128]{2,1,0:T(8,128)(2,1)} %get-tuple-element.223), kind=kOutput, calls=%fused_computation.4.clone.1 | convolution fusion | flops 407369728 | bytes 13321216 | tf_op jit(solution)/shard_map/while/body/eval_jaxpr/rgd,kd->grk/dot_general | solution.py:27
  101.3 10.6 %dynamic_update_slice.19 = f32[2,768,128]{2,0,1:T(2,128)} dynamic-update-slice(f32[2,768,128]{2,0,1:T(2,128)} %get-tuple-element.206, f32[1,768,128]{2,0,1:T(1,128)S(1)} %bitcast.146, s32[]{:T(128)} %get-tuple-element.204, s32[]{:T(128)} %constant.13.clone.1..sunk, s32[]{:T(128)} %constant.13.clone.1..sunk) | dynamic-update-slice | bytes 786436 | tf_op jit(solution)/shard_map/while/body/jit(dynamic_update_index_in_dim)/dynamic_update_slice | solution.py:53
  114.2 4.0 %fusion.101 = f32[768,128,1]{1,0,2:T(8,128)S(1)} fusion(bf16[2,256,8,128]{3,1,2,0:T(8,128)(2,1)} %copy-done.3, s32[]{:T(128)} %get-tuple-element.204, f32[8,256,768]{1,2,0:T(8,128)} %get-tuple-element.187, f32[8,256]{1,0:T(8,128)S(1)} %get-tuple-element.188), kind=kOutput, calls=%fused_computation.10.clone.1 | convolution fusion | flops 405798912 | bytes 7217664 | tf_op jit(solution)/shard_map/while/body/eval_jaxpr/grk,rgd->kd/dot_general | solution.py:24
  118.2 8.6 %dynamic_update_slice.20 = f32[2,768,128]{2,0,1:T(2,128)S(1)} dynamic-update-slice(f32[2,768,128]{2,0,1:T(2,128)S(1)} %copy-done.5, f32[1,768,128]{2,0,1:T(1,128)S(1)} %bitcast.148, s32[]{:T(128)} %get-tuple-element.204, s32[]{:T(128)} %constant.13.clone.1..sunk, s32[]{:T(128)} %constant.13.clone.1..sunk) | dynamic-update-slice | bytes 786436 | tf_op jit(solution)/shard_map/while/body/jit(dynamic_update_index_in_dim)/dynamic_update_slice | solution.py:53
  127.6 2.6 %copy.57 = bf16[256,2,8,128]{3,2,1,0:T(8,128)(2,1)} copy(bf16[256,2,8,128]{0,3,2,1:T(8,128)(2,1)} %bitcast.152) | data formatting | bytes 2097152 | tf_op jit(solution)/shard_map/convert_element_type | solution.py:90
  130.3 3.5 %all-to-all-start.2 = ((bf16[256,16,128]{2,1,0:T(8,128)(2,1)}), bf16[256,16,128]{2,1,0:T(8,128)(2,1)S(1)}, u32[]{:S(2)}, u32[]{:S(2)}) async-start(bf16[256,16,128]{2,1,0:T(8,128)(2,1)} %bitcast.13), calls=%async_computation.2 | async-start | bytes 2097152 | tf_op jit(solution)/shard_map/all_to_all | solution.py:89
  141.1 8.1 %collective-permute-done.6 = f32[256,2,128]{2,1,0:T(2,128)S(1)} collective-permute-done((f32[256,2,128]{2,1,0:T(2,128)S(1)}, f32[256,2,128]{2,1,0:T(2,128)S(1)}, u32[]{:S(2)}, u32[]{:S(2)}) %collective-permute-start.6) | collective-permute-done | bytes 262176 | tf_op jit(solution)/shard_map/ppermute | solution.py:10
  149.2 13.1 %collective-permute-done.7 = f32[256,2,128]{2,1,0:T(2,128)S(1)} collective-permute-done((f32[256,2,128]{2,1,0:T(2,128)S(1)}, f32[256,2,128]{2,1,0:T(2,128)S(1)}, u32[]{:S(2)}, u32[]{:S(2)}) %collective-permute-start.7) | collective-permute-done | bytes 262176 | tf_op jit(solution)/shard_map/ppermute | solution.py:10
  164.1 14.8 %collective-permute-done.5 = f32[256,2,128]{2,1,0:T(2,128)S(1)} collective-permute-done((f32[256,2,128]{2,1,0:T(2,128)S(1)}, f32[256,2,128]{2,1,0:T(2,128)S(1)}, u32[]{:S(2)}, u32[]{:S(2)}) %collective-permute-start.5) | collective-permute-done | bytes 262176 | tf_op jit(solution)/shard_map/ppermute | solution.py:10
  (70 shorter events, 34.4 us)
Async XLA Ops:
  0.6 25.1 %copy-start.7 = (bf16[256,2,128]{2,1,0:T(2,128)(2,1)S(1)}, bf16[256,2,128]{2,1,0:T(2,128)(2,1)}, u32[]{:S(2)}) copy-start(bf16[256,2,128]{2,1,0:T(2,128)(2,1)} %param.7) | copy-start | bytes 393220
  0.6 33.9 %copy-start.8 = (bf16[256,2,128]{2,1,0:T(2,128)(2,1)S(1)}, bf16[256,2,128]{2,1,0:T(2,128)(2,1)}, u32[]{:S(2)}) copy-start(bf16[256,2,128]{2,1,0:T(2,128)(2,1)} %param.8) | copy-start | bytes 393220
  3.6 18.7 %all-to-all-start.1 = ((bf16[64,64,128]{2,0,1:T(8,128)(2,1)}), bf16[64,64,128]{2,0,1:T(8,128)(2,1)S(1)}, u32[]{:S(2)}, u32[]{:S(2)}) async-start(bf16[64,64,128]{2,0,1:T(8,128)(2,1)} %copy.55), calls=%async_computation.1 | async-start | bytes 2097152 | tf_op jit(solution)/shard_map/all_to_all | solution.py:75
  22.2 23.3 %all-to-all-start = ((bf16[4,64,16,128]{3,2,1,0:T(8,128)(2,1)}), bf16[4,64,16,128]{3,2,1,0:T(8,128)(2,1)S(1)}, u32[]{:S(2)}, u32[]{:S(2)}) async-start(bf16[4,64,16,128]{3,2,1,0:T(8,128)(2,1)} %pad_maximum_fusion), calls=%async_computation | async-start | bytes 2097152 | tf_op jit(solution)/shard_map/all_to_all | solution.py:70
  25.8 17.0 %collective-permute-start = (bf16[256,2,128]{2,0,1:T(8,128)(2,1)S(1)}, bf16[256,2,128]{2,0,1:T(8,128)(2,1)S(1)}, u32[]{:S(2)}, u32[]{:S(2)}) collective-permute-start(bf16[256,2,128]{2,0,1:T(8,128)(2,1)S(1)} %copy.48), channel_id=1, source_target_pairs={{0,8},{4,12},{8,16},{12,20},{16,24},{20,28},{1,9},{5,13},{9,17},{1... | collective-permute-start | bytes 393224 | tf_op jit(solution)/shard_map/ppermute | solution.py:10
  31.0 11.7 %collective-permute-start.1 = (bf16[256,2,128]{2,0,1:T(8,128)(2,1)S(1)}, bf16[256,2,128]{2,0,1:T(8,128)(2,1)S(1)}, u32[]{:S(2)}, u32[]{:S(2)}) collective-permute-start(bf16[256,2,128]{2,0,1:T(8,128)(2,1)S(1)} %copy.48), channel_id=1, source_target_pairs={{0,4},{4,8},{8,12},{12,16},{16,20},{20,24},{24,28},{1,5},{5,9},{9,... | collective-permute-start | bytes 393224 | tf_op jit(solution)/shard_map/ppermute | solution.py:10
  34.6 9.0 %collective-permute-start.2 = (bf16[256,2,128]{2,0,1:T(8,128)(2,1)S(1)}, bf16[256,2,128]{2,0,1:T(8,128)(2,1)S(1)}, u32[]{:S(2)}, u32[]{:S(2)}) collective-permute-start(bf16[256,2,128]{2,0,1:T(8,128)(2,1)S(1)} %copy.52), channel_id=1, source_target_pairs={{0,8},{4,12},{8,16},{12,20},{16,24},{20,28},{1,9},{5,13},{9,17},{1... | collective-permute-start | bytes 393224 | tf_op jit(solution)/shard_map/ppermute | solution.py:10
  37.8 6.9 %collective-permute-start.3 = (bf16[256,2,128]{2,0,1:T(8,128)(2,1)S(1)}, bf16[256,2,128]{2,0,1:T(8,128)(2,1)S(1)}, u32[]{:S(2)}, u32[]{:S(2)}) collective-permute-start(bf16[256,2,128]{2,0,1:T(8,128)(2,1)S(1)} %copy.52), channel_id=1, source_target_pairs={{0,4},{4,8},{8,12},{12,16},{16,20},{20,24},{24,28},{1,5},{5,9},{9,... | collective-permute-start | bytes 393224 | tf_op jit(solution)/shard_map/ppermute | solution.py:10
  45.9 10.7 %copy-start.1 = (bf16[2,256,8,128]{3,1,2,0:T(8,128)(2,1)}, bf16[2,256,8,128]{3,1,2,0:T(8,128)(2,1)S(1)}, u32[]{:S(2)}) copy-start(bf16[2,256,8,128]{3,1,2,0:T(8,128)(2,1)S(1)} %get-tuple-element.222) | copy-start | bytes 3145732 | tf_op jit(solution)/shard_map/while
  45.9 10.7 %copy-start.3 = (bf16[2,256,8,128]{3,1,2,0:T(8,128)(2,1)}, bf16[2,256,8,128]{3,1,2,0:T(8,128)(2,1)S(1)}, u32[]{:S(2)}) copy-start(bf16[2,256,8,128]{3,1,2,0:T(8,128)(2,1)S(1)} %get-tuple-element.224) | copy-start | bytes 3145732 | tf_op jit(solution)/shard_map/while
  52.5 4.7 %copy-start = (f32[8,256,768]{1,2,0:T(8,128)S(1)}, f32[8,256,768]{1,2,0:T(8,128)}, u32[]{:S(2)}) copy-start(f32[8,256,768]{1,2,0:T(8,128)} %get-tuple-element.187) | copy-start | bytes 18874372 | tf_op jit(solution)/shard_map/while
  73.3 4.0 %copy-start.5 = (f32[2,768,128]{2,0,1:T(2,128)S(1)}, f32[2,768,128]{2,0,1:T(2,128)}, u32[]{:S(2)}) copy-start(f32[2,768,128]{2,0,1:T(2,128)} %get-tuple-element.207) | copy-start | bytes 2359300 | tf_op jit(solution)/shard_map/while
  73.3 13.4 %copy-start.2 = (bf16[2,256,8,128]{3,1,2,0:T(8,128)(2,1)S(1)}, bf16[2,256,8,128]{3,1,2,0:T(8,128)(2,1)}, u32[]{:S(2)}) copy-start(bf16[2,256,8,128]{3,1,2,0:T(8,128)(2,1)} %copy-done.1) | copy-start | bytes 3145732 | tf_op jit(solution)/shard_map/while
  73.3 13.4 %copy-start.4 = (bf16[2,256,8,128]{3,1,2,0:T(8,128)(2,1)S(1)}, bf16[2,256,8,128]{3,1,2,0:T(8,128)(2,1)}, u32[]{:S(2)}) copy-start(bf16[2,256,8,128]{3,1,2,0:T(8,128)(2,1)} %copy-done.3) | copy-start | bytes 3145732 | tf_op jit(solution)/shard_map/while
  86.8 10.7 %copy-start.1 = (bf16[2,256,8,128]{3,1,2,0:T(8,128)(2,1)}, bf16[2,256,8,128]{3,1,2,0:T(8,128)(2,1)S(1)}, u32[]{:S(2)}) copy-start(bf16[2,256,8,128]{3,1,2,0:T(8,128)(2,1)S(1)} %get-tuple-element.222) | copy-start | bytes 3145732 | tf_op jit(solution)/shard_map/while
  86.8 10.7 %copy-start.3 = (bf16[2,256,8,128]{3,1,2,0:T(8,128)(2,1)}, bf16[2,256,8,128]{3,1,2,0:T(8,128)(2,1)S(1)}, u32[]{:S(2)}) copy-start(bf16[2,256,8,128]{3,1,2,0:T(8,128)(2,1)S(1)} %get-tuple-element.224) | copy-start | bytes 3145732 | tf_op jit(solution)/shard_map/while
  93.4 4.7 %copy-start = (f32[8,256,768]{1,2,0:T(8,128)S(1)}, f32[8,256,768]{1,2,0:T(8,128)}, u32[]{:S(2)}) copy-start(f32[8,256,768]{1,2,0:T(8,128)} %get-tuple-element.187) | copy-start | bytes 18874372 | tf_op jit(solution)/shard_map/while
  114.2 13.4 %copy-start.2 = (bf16[2,256,8,128]{3,1,2,0:T(8,128)(2,1)S(1)}, bf16[2,256,8,128]{3,1,2,0:T(8,128)(2,1)}, u32[]{:S(2)}) copy-start(bf16[2,256,8,128]{3,1,2,0:T(8,128)(2,1)} %copy-done.1) | copy-start | bytes 3145732 | tf_op jit(solution)/shard_map/while
  114.2 13.4 %copy-start.4 = (bf16[2,256,8,128]{3,1,2,0:T(8,128)(2,1)S(1)}, bf16[2,256,8,128]{3,1,2,0:T(8,128)(2,1)}, u32[]{:S(2)}) copy-start(bf16[2,256,8,128]{3,1,2,0:T(8,128)(2,1)} %copy-done.3) | copy-start | bytes 3145732 | tf_op jit(solution)/shard_map/while
  130.3 50.5 %all-to-all-start.2 = ((bf16[256,16,128]{2,1,0:T(8,128)(2,1)}), bf16[256,16,128]{2,1,0:T(8,128)(2,1)S(1)}, u32[]{:S(2)}, u32[]{:S(2)}) async-start(bf16[256,16,128]{2,1,0:T(8,128)(2,1)} %bitcast.13), calls=%async_computation.2 | async-start | bytes 2097152 | tf_op jit(solution)/shard_map/all_to_all | solution.py:89
  134.9 14.3 %collective-permute-start.6 = (f32[256,2,128]{2,1,0:T(2,128)S(1)}, f32[256,2,128]{2,1,0:T(2,128)S(1)}, u32[]{:S(2)}, u32[]{:S(2)}) collective-permute-start(f32[256,2,128]{2,1,0:T(2,128)S(1)} %get-tuple-element.112), channel_id=1, source_target_pairs={{4,0},{8,4},{12,8},{16,12},{20,16},{24,20},{28,24},{5,1},{9,5},{13... | collective-permute-start | bytes 786440 | tf_op jit(solution)/shard_map/ppermute | solution.py:10
  136.2 26.2 %collective-permute-start.7 = (f32[256,2,128]{2,1,0:T(2,128)S(1)}, f32[256,2,128]{2,1,0:T(2,128)S(1)}, u32[]{:S(2)}, u32[]{:S(2)}) collective-permute-start(f32[256,2,128]{2,1,0:T(2,128)S(1)} %get-tuple-element.113), channel_id=1, source_target_pairs={{8,0},{12,4},{16,8},{20,12},{24,16},{28,20},{9,1},{13,5},{17,9},{2... | collective-permute-start | bytes 786440 | tf_op jit(solution)/shard_map/ppermute | solution.py:10
  138.5 25.6 %collective-permute-start.4 = (f32[256,2,128]{2,1,0:T(2,128)S(1)}, f32[256,2,128]{2,1,0:T(2,128)S(1)}, u32[]{:S(2)}, u32[]{:S(2)}) collective-permute-start(f32[256,2,128]{2,1,0:T(2,128)S(1)} %get-tuple-element.114), channel_id=1, source_target_pairs={{4,0},{8,4},{12,8},{16,12},{20,16},{24,20},{28,24},{5,1},{9,5},{13... | collective-permute-start | bytes 786440 | tf_op jit(solution)/shard_map/ppermute | solution.py:10
  139.8 39.1 %collective-permute-start.5 = (f32[256,2,128]{2,1,0:T(2,128)S(1)}, f32[256,2,128]{2,1,0:T(2,128)S(1)}, u32[]{:S(2)}, u32[]{:S(2)}) collective-permute-start(f32[256,2,128]{2,1,0:T(2,128)S(1)} %get-tuple-element.115), channel_id=1, source_target_pairs={{8,0},{12,4},{16,8},{20,12},{24,16},{28,20},{9,1},{13,5},{17,9},{2... | collective-permute-start | bytes 786440 | tf_op jit(solution)/shard_map/ppermute | solution.py:10
  (3 other events, 5.7 us)
